TPU v7x, 32 devices: a 4x2x2 block of a 4x4x8 slice. The times are simulated.
32 devices in a mesh: rep: 4 (over y, z), data: 8 (over x, core).
Axes of the slice: x: 4, y: 2, z: 2, core: 2. Of those that a mesh axis runs over, the one named last changes fastest.
The devices are a block of a 4x4x8 slice.
Arguments:
- x: bfloat16 [2048, 2048], P(('rep', 'data')), parts along dimension 0
- adapter_id: int32 [2048], P(('rep', 'data')), parts along dimension 0
- w_gate: bfloat16 [2048, 5632], replicated
- w_up: bfloat16 [2048, 5632], replicated
- w_down: bfloat16 [5632, 2048], replicated
- a_gate: bfloat16 [1024, 8, 2048], P('data')
- b_gate: bfloat16 [1024, 8, 5632], P('data')
- a_up: bfloat16 [1024, 8, 2048], P('data')
- b_up: bfloat16 [1024, 8, 5632], P('data')
- a_down: bfloat16 [1024, 8, 5632], P('data')
- b_down: bfloat16 [1024, 8, 2048], P('data')
Outputs:
- output: bfloat16 [2048, 2048], P(('rep', 'data')), parts along dimension 0
There are 4 independent parts. A program takes and returns all parts, laid end to end along the dimension named above; an argument that names none is the same for every part.
All inputs are finite; a program needn't handle non-finite values.
Results may differ from a plain program's by a relative error of at most 0.00571596.
Values are sent between devices in bfloat16 or wider.
A program may use at most 768 MiB of HBM per device.

v0:
```python
import jax
import jax.numpy as jnp
from jax import lax
from jax.sharding import PartitionSpec as P, NamedSharding

value_a10 = 32


def value_a9(tok_rows, row_ids, a_mat, b_mat):
    array_b10 = value_a10 / a_mat.shape[1]
    a_rows = jnp.take(a_mat, row_ids, axis=0)
    b_rows = jnp.take(b_mat, row_ids, axis=0)
    low_rank = jnp.einsum("md,mrd->mr", tok_rows, a_rows, preferred_element_type=jnp.float32).astype(jnp.bfloat16)
    full_rows = jnp.einsum("ns,nsg->ng", low_rank, b_rows, preferred_element_type=jnp.float32)
    return (array_b10 * full_rows).astype(jnp.bfloat16)


def solution(mesh):
    groups = mesh.shape["data"]
    row_spec = P(("rep", "data"), None)
    id_spec = P(("rep", "data"))
    owned_spec = P("data", None, None)

    def device_step(x, adapter_id, w_gate, w_up, w_down, a_gate, b_gate, a_up, b_up, a_down, b_down):
        tok_count = x.shape[0]
        per_owner = a_gate.shape[0]
        capacity = (3 * tok_count + groups - 1) // groups
        owner_idx = adapter_id // per_owner
        local_ad = adapter_id % per_owner
        owner_hot = (owner_idx[:, None] == jnp.arange(groups)[None, :]).astype(jnp.int32)
        arrival = jnp.sum(jnp.cumsum(owner_hot, axis=0) * owner_hot, axis=1) - 1
        slot_idx = owner_idx * capacity + arrival
        slot_hot = (slot_idx[:, None] == jnp.arange(groups * capacity)[None, :]).astype(jnp.int32)
        dispatch = slot_hot.astype(jnp.bfloat16)
        send_ids = jnp.sum(slot_hot * local_ad[:, None], axis=0)
        send_x = jnp.einsum("tm,td->md", dispatch, x, preferred_element_type=jnp.float32).astype(jnp.bfloat16)
        recv_ids = lax.all_to_all(send_ids, "data", 0, 0, tiled=True)
        recv_x = lax.all_to_all(send_x, "data", 0, 0, tiled=True)
        gate_back = lax.all_to_all(value_a9(recv_x, recv_ids, a_gate, b_gate), "data", 0, 0, tiled=True)
        up_back = lax.all_to_all(value_a9(recv_x, recv_ids, a_up, b_up), "data", 0, 0, tiled=True)
        gate_pre = jnp.dot(x, w_gate, preferred_element_type=jnp.float32) + jnp.einsum("tm,mf->tf", dispatch, gate_back, preferred_element_type=jnp.float32)
        up_pre = jnp.dot(x, w_up, preferred_element_type=jnp.float32) + jnp.einsum("tm,mf->tf", dispatch, up_back, preferred_element_type=jnp.float32)
        hidden = (jax.nn.silu(gate_pre) * up_pre).astype(jnp.bfloat16)
        send_h = jnp.einsum("tm,tf->mf", dispatch, hidden, preferred_element_type=jnp.float32).astype(jnp.bfloat16)
        recv_h = lax.all_to_all(send_h, "data", 0, 0, tiled=True)
        down_back = lax.all_to_all(value_a9(recv_h, recv_ids, a_down, b_down), "data", 0, 0, tiled=True)
        down_out = jnp.dot(hidden, w_down, preferred_element_type=jnp.float32) + jnp.einsum("tm,md->td", dispatch, down_back, preferred_element_type=jnp.float32)
        return (x.astype(jnp.float32) + down_out).astype(jnp.bfloat16)

    return jax.shard_map(device_step, mesh=mesh, in_specs=(row_spec, id_spec, P(), P(), P(), owned_spec, owned_spec, owned_spec, owned_spec, owned_spec, owned_spec), out_specs=row_spec, check_vma=False)
```

profile of v0, /device:TPU:81, one launch (start us, length us, event | category | flops | bytes accessed | tf_op | source)
XLA Modules:
  0.0 265.8 jit_solution(7145006482849134333)
XLA Ops:
  1.8 6.0 %all-to-all-start.1 = ((s32[8,24,1]{1,2,0:T(1,128)}), s32[8,24,1]{1,2,0:T(1,128)S(1)}, u32[]{:S(2)}, u32[]{:S(2)}) async-start(s32[8,24,1]{1,2,0:T(1,128)} %bitcast.3), calls=%async_computation.1 | async-start | bytes 8192 | tf_op jit(solution)/shard_map/all_to_all | solution.py:37
  7.8 2.3 convolution_convert_fusion.1
  12.2 4.2 %all-to-all-start = ((bf16[8,24,2048]{2,1,0:T(8,128)(2,1)}), bf16[8,24,2048]{2,1,0:T(8,128)(2,1)S(1)}, u32[]{:S(2)}, u32[]{:S(2)}) async-start(bf16[8,24,2048]{2,1,0:T(8,128)(2,1)} %bitcast), calls=%async_computation | async-start | bytes 1572864 | tf_op jit(solution)/shard_map/all_to_all | solution.py:38
  17.7 10.1 %gather_fusion = bf16[192,8,2048]{2,1,0:T(8,128)(2,1)} fusion(bf16[128,8,2048]{2,1,0:T(8,128)(2,1)} %param.20, s32[1024]{0:T(1024)S(1)} %pad_clamp_fusion), kind=kCustom, calls=%fused_computation.clone | custom fusion | bytes 12583680 | tf_op jit(solution)/shard_map/jit(_take)/gather | solution.py:11
  27.8 13.7 %gather_fusion.1 = bf16[192,8,5632]{2,1,0:T(8,128)(2,1)} fusion(bf16[128,8,5632]{2,1,0:T(8,128)(2,1)} %param.21, s32[1024]{0:T(1024)S(1)} %pad_clamp_fusion), kind=kCustom, calls=%fused_computation.1.clone | custom fusion | bytes 34603776 | tf_op jit(solution)/shard_map/jit(_take)/gather | solution.py:12
  41.5 10.1 %gather_fusion.2 = bf16[192,8,2048]{2,1,0:T(8,128)(2,1)} fusion(bf16[128,8,2048]{2,1,0:T(8,128)(2,1)} %param.22, s32[1024]{0:T(1024)S(1)} %pad_clamp_fusion), kind=kCustom, calls=%fused_computation.2.clone | custom fusion | bytes 12583680 | tf_op jit(solution)/shard_map/jit(_take)/gather | solution.py:11
  51.6 13.7 %gather_fusion.3 = bf16[192,8,5632]{2,1,0:T(8,128)(2,1)} fusion(bf16[128,8,5632]{2,1,0:T(8,128)(2,1)} %param.23, s32[1024]{0:T(1024)S(1)} %pad_clamp_fusion), kind=kCustom, calls=%fused_computation.4.clone | custom fusion | bytes 34603776 | tf_op jit(solution)/shard_map/jit(_take)/gather | solution.py:12
  65.3 7.5 %fusion.18 = f32[192,1,8]{2,1,0:T(1,128)S(1)} fusion(bf16[192,8,2048]{2,1,0:T(8,128)(2,1)} %gather_fusion, pred[192]{0:T(512)(128)(4,1)S(1)} %compare_and_fusion, bf16[192,2048,1]{1,0,2:T(8,128)(2,1)S(1)} %bitcast.54), kind=kOutput, calls=%fused_computation.27 | convolution fusion | flops 9437184 | bytes 7084224 | tf_op jit(solution)/shard_map/md,mrd->mr/dot_general | solution.py:13
  72.8 19.3 %fusion.4 = f32[192,1,5632]{2,1,0:T(1,128)S(1)} fusion(bf16[192,8,5632]{2,1,0:T(8,128)(2,1)} %gather_fusion.1, pred[192]{0:T(512)(128)(4,1)S(1)} %compare_and_fusion, bf16[192,8,1]{1,0,2:T(8,128)(2,1)S(1)} %convert_bitcast_fusion.2), kind=kOutput, calls=%fused_computation.10 | convolution fusion | flops 25952256 | bytes 21630144 | tf_op jit(solution)/shard_map/ns,nsg->ng/dot_general | solution.py:14
  93.8 5.6 %all-to-all-start.2 = ((bf16[8,24,5632]{2,1,0:T(8,128)(2,1)}), bf16[8,24,5632]{2,1,0:T(8,128)(2,1)S(1)}, u32[]{:S(2)}, u32[]{:S(2)}) async-start(bf16[8,24,5632]{2,1,0:T(8,128)(2,1)} %bitcast.8), calls=%async_computation.2 | async-start | bytes 4325376 | tf_op jit(solution)/shard_map/all_to_all | solution.py:39
  99.4 7.5 %fusion.16 = f32[192,1,8]{2,1,0:T(1,128)S(1)} fusion(bf16[192,8,2048]{2,1,0:T(8,128)(2,1)} %gather_fusion.2, pred[192]{0:T(512)(128)(4,1)S(1)} %compare_and_fusion, bf16[192,2048,1]{1,0,2:T(8,128)(2,1)S(1)} %bitcast.55), kind=kOutput, calls=%fused_computation.25 | convolution fusion | flops 9437184 | bytes 7084224 | tf_op jit(solution)/shard_map/md,mrd->mr/dot_general | solution.py:13
  106.9 8.8 %fusion.2 = f32[192,1,5632]{2,1,0:T(1,128)S(1)} fusion(bf16[192,8,5632]{2,1,0:T(8,128)(2,1)} %gather_fusion.3, pred[192]{0:T(512)(128)(4,1)S(1)} %compare_and_fusion, bf16[192,8,1]{1,0,2:T(8,128)(2,1)S(1)} %convert_bitcast_fusion.1), kind=kOutput, calls=%fused_computation.8 | convolution fusion | flops 25952256 | bytes 21630144 | tf_op jit(solution)/shard_map/ns,nsg->ng/dot_general | solution.py:14
  117.4 8.7 %all-to-all-done.2 = bf16[8,24,5632]{2,1,0:T(8,128)(2,1)S(1)} async-done(((bf16[8,24,5632]{2,1,0:T(8,128)(2,1)}), bf16[8,24,5632]{2,1,0:T(8,128)(2,1)S(1)}, u32[]{:S(2)}, u32[]{:S(2)}) %all-to-all-start.2) | async-done | bytes 2162720 | tf_op jit(solution)/shard_map/all_to_all | solution.py:39
  126.1 5.4 %all-to-all-start.3 = ((bf16[8,24,5632]{2,1,0:T(8,128)(2,1)}), bf16[8,24,5632]{2,1,0:T(8,128)(2,1)}, u32[]{:S(2)}, u32[]{:S(2)}) async-start(bf16[8,24,5632]{2,1,0:T(8,128)(2,1)} %bitcast.14), calls=%async_computation.3 | async-start | bytes 4325376 | tf_op jit(solution)/shard_map/all_to_all | solution.py:40
  133.3 25.2 %all-to-all-done.3 = bf16[8,24,5632]{2,1,0:T(8,128)(2,1)} async-done(((bf16[8,24,5632]{2,1,0:T(8,128)(2,1)}), bf16[8,24,5632]{2,1,0:T(8,128)(2,1)}, u32[]{:S(2)}, u32[]{:S(2)}) %all-to-all-start.3) | async-done | bytes 2162720 | tf_op jit(solution)/shard_map/all_to_all | solution.py:40
  160.6 12.0 %convolution_add_fusion.1 = f32[64,5632]{1,0:T(8,128)S(1)} fusion(f32[64,5632]{1,0:T(8,128)} %fusion.39, bf16[64,2048]{1,0:T(8,128)(2,1)S(1)} %copy-done.1, bf16[2048,5632]{1,0:T(8,128)(2,1)} %param.17), kind=kOutput, calls=%fused_computation.20 | convolution fusion | flops 1476755456 | bytes 26214400 | tf_op jit(solution)/shard_map/dot_general | solution.py:41
  172.6 11.9 %fusion.13 = bf16[64,5632]{1,0:T(8,128)(2,1)S(1)} fusion(f32[64,5632]{1,0:T(8,128)S(1)} %fusion.38, bf16[64,2048]{1,0:T(8,128)(2,1)S(1)} %copy-done.1, bf16[2048,5632]{1,0:T(8,128)(2,1)} %param.18, f32[64,5632]{1,0:T(8,128)S(1)} %convolution_add_fusion.1), kind=kOutput, calls=%fused_computation.22 | convolution fusion | flops 1478918144 | bytes 26935296 | tf_op jit(solution)/shard_map/dot_general | solution.py:42
  186.8 5.3 %all-to-all-start.4 = ((bf16[8,24,5632]{2,1,0:T(8,128)(2,1)}), bf16[8,24,5632]{2,1,0:T(8,128)(2,1)}, u32[]{:S(2)}, u32[]{:S(2)}) async-start(bf16[8,24,5632]{2,1,0:T(8,128)(2,1)} %bitcast.16), calls=%async_computation.4 | async-start | bytes 4325376 | tf_op jit(solution)/shard_map/all_to_all | solution.py:45
  192.1 13.7 %gather_fusion.4 = bf16[192,8,5632]{2,1,0:T(8,128)(2,1)} fusion(bf16[128,8,5632]{2,1,0:T(8,128)(2,1)} %param.24, s32[1024]{0:T(1024)S(1)} %pad_clamp_fusion), kind=kCustom, calls=%fused_computation.5.clone | custom fusion | bytes 34603776 | tf_op jit(solution)/shard_map/jit(_take)/gather | solution.py:11
  205.8 10.1 %gather_fusion.5 = bf16[192,8,2048]{2,1,0:T(8,128)(2,1)} fusion(bf16[128,8,2048]{2,1,0:T(8,128)(2,1)} %param.25, s32[1024]{0:T(1024)S(1)} %pad_clamp_fusion), kind=kCustom, calls=%fused_computation.3.clone | custom fusion | bytes 12583680 | tf_op jit(solution)/shard_map/jit(_take)/gather | solution.py:12
  215.9 3.1 %all-to-all-done.4 = bf16[8,24,5632]{2,1,0:T(8,128)(2,1)} async-done(((bf16[8,24,5632]{2,1,0:T(8,128)(2,1)}), bf16[8,24,5632]{2,1,0:T(8,128)(2,1)}, u32[]{:S(2)}, u32[]{:S(2)}) %all-to-all-start.4) | async-done | bytes 2162720 | tf_op jit(solution)/shard_map/all_to_all | solution.py:45
  219.0 17.2 %fusion = f32[192,1,8]{2,1,0:T(1,128)S(1)} fusion(bf16[192,8,5632]{2,1,0:T(8,128)(2,1)} %gather_fusion.4, pred[192]{0:T(512)(128)(4,1)S(1)} %compare_and_fusion, bf16[192,5632,1]{1,0,2:T(8,128)(2,1)} %bitcast.18), kind=kOutput, calls=%fused_computation.6 | convolution fusion | flops 25952256 | bytes 19470528 | tf_op jit(solution)/shard_map/md,mrd->mr/dot_general | solution.py:13
  238.9 15.7 %all_to_all.72 = bf16[8,24,2048]{2,1,0:T(8,128)(2,1)S(1)} all-to-all(bf16[8,24,2048]{2,1,0:T(8,128)(2,1)S(1)} %bitcast.53), channel_id=1, replica_groups=mesh['rep'=4,'data'=8] {'data'}, dimensions={0} | all-to-all | bytes 1572864 | tf_op jit(solution)/shard_map/all_to_all | solution.py:46
  254.9 10.5 %fusion.30 = bf16[64,2048]{1,0:T(8,128)(2,1)} fusion(f32[64,2048]{1,0:T(8,128)S(1)} %fusion.37, bf16[64,5632]{1,0:T(8,128)(2,1)S(1)} %fusion.13, bf16[5632,2048]{1,0:T(8,128)(2,1)} %param.19, bf16[64,2048]{1,0:T(8,128)(2,1)S(1)} %copy-done.1), kind=kOutput, calls=%fused_computation.43 | convolution fusion | flops 1476919296 | bytes 24838144 | tf_op jit(solution)/shard_map/dot_general | solution.py:47
  (30 shorter events, 17.8 us)
Async XLA Ops:
  1.8 10.4 %all-to-all-start.1 = ((s32[8,24,1]{1,2,0:T(1,128)}), s32[8,24,1]{1,2,0:T(1,128)S(1)}, u32[]{:S(2)}, u32[]{:S(2)}) async-start(s32[8,24,1]{1,2,0:T(1,128)} %bitcast.3), calls=%async_computation.1 | async-start | bytes 8192 | tf_op jit(solution)/shard_map/all_to_all | solution.py:37
  12.2 53.1 %all-to-all-start = ((bf16[8,24,2048]{2,1,0:T(8,128)(2,1)}), bf16[8,24,2048]{2,1,0:T(8,128)(2,1)S(1)}, u32[]{:S(2)}, u32[]{:S(2)}) async-start(bf16[8,24,2048]{2,1,0:T(8,128)(2,1)} %bitcast), calls=%async_computation | async-start | bytes 1572864 | tf_op jit(solution)/shard_map/all_to_all | solution.py:38
  93.8 32.3 %all-to-all-start.2 = ((bf16[8,24,5632]{2,1,0:T(8,128)(2,1)}), bf16[8,24,5632]{2,1,0:T(8,128)(2,1)S(1)}, u32[]{:S(2)}, u32[]{:S(2)}) async-start(bf16[8,24,5632]{2,1,0:T(8,128)(2,1)} %bitcast.8), calls=%async_computation.2 | async-start | bytes 4325376 | tf_op jit(solution)/shard_map/all_to_all | solution.py:39
  117.4 43.3 %copy-start.1 = (bf16[64,2048]{1,0:T(8,128)(2,1)S(1)}, bf16[64,2048]{1,0:T(8,128)(2,1)}, u32[]{:S(2)}) copy-start(bf16[64,2048]{1,0:T(8,128)(2,1)} %param.15) | copy-start | bytes 786436
  126.1 32.3 %all-to-all-start.3 = ((bf16[8,24,5632]{2,1,0:T(8,128)(2,1)}), bf16[8,24,5632]{2,1,0:T(8,128)(2,1)}, u32[]{:S(2)}, u32[]{:S(2)}) async-start(bf16[8,24,5632]{2,1,0:T(8,128)(2,1)} %bitcast.14), calls=%async_computation.3 | async-start | bytes 4325376 | tf_op jit(solution)/shard_map/all_to_all | solution.py:40
  186.8 32.2 %all-to-all-start.4 = ((bf16[8,24,5632]{2,1,0:T(8,128)(2,1)}), bf16[8,24,5632]{2,1,0:T(8,128)(2,1)}, u32[]{:S(2)}, u32[]{:S(2)}) async-start(bf16[8,24,5632]{2,1,0:T(8,128)(2,1)} %bitcast.16), calls=%async_computation.4 | async-start | bytes 4325376 | tf_op jit(solution)/shard_map/all_to_all | solution.py:45
  219.0 17.2 %copy-start = (bf16[192,8,2048]{2,1,0:T(8,128)(2,1)S(1)}, bf16[192,8,2048]{2,1,0:T(8,128)(2,1)}, u32[]{:S(2)}) copy-start(bf16[192,8,2048]{2,1,0:T(8,128)(2,1)} %gather_fusion.5) | copy-start | bytes 18874372
where the time goes:
time: 271 us; the launch traced here: 266 us
  matrix products  105 us (39%)
  local copies, waits for them, and re-layouts  72.7 us (27%)
  waiting for transfers between devices  39.2 us (14%)
  starting transfers between devices  26.5 us (10%)
  blocking collectives  15.7 us (6%)
  other arithmetic  5.74 us (2%)
    gather x3, local copies, waits for them, and re-layouts, value_a9(): b_rows = jnp.take(b_mat, row_ids, axis=0)  37.5 us
    gather x3, local copies, waits for them, and re-layouts, value_a9(): a_rows = jnp.take(a_mat, row_ids, axis=0)  33.9 us
    dot_general x3, matrix products, value_a9(): jnp.einsum('md,mrd->mr', tok_rows, a_rows, preferred_element_type=jnp.flo...  32.1 us
    dot_general x3, matrix products, value_a9(): jnp.einsum('ns,nsg->ng', low_rank, b_rows, preferred_element_type=jnp.flo...  30.3 us
    all_to_all x1, waiting for transfers between devices, device_step(): lax.all_to_all(value_a9(recv_x, recv_ids, a_up, b_up), 'data', 0, 0, tile...  25.2 us
    all_to_all x1, blocking collectives, device_step(): lax.all_to_all(value_a9(recv_h, recv_ids, a_down, b_down), 'data', 0, 0,...  15.7 us
    dot_general x1, matrix products, device_step(): jnp.dot(x, w_gate, preferred_element_type=jnp.float32)  12 us
    dot_general x1, matrix products, device_step(): jnp.dot(x, w_up, preferred_element_type=jnp.float32)  11.9 us
  transfers between devices with their start and end apart: 5, of which 4 were waited for; matrix products, arithmetic and copies ran while one was open for 36% of the time, Pallas kernels for 0%

commit v1 on v0

v1 whole, which is shorter than its diff:
```python
import functools

import jax
import jax.numpy as jnp
from jax import lax
from jax.experimental import pallas as pl
from jax.experimental.pallas import tpu as pltpu
from jax.sharding import PartitionSpec as P

LORA_ALPHA = 32
F32 = jnp.float32
BF16 = jnp.bfloat16
MESH = pl.DeviceIdType.MESH

KC = 512
FT = 512
NT = 256
W_SLOTS = 3
S_SLOTS = 12
D_SLOTS = 4


def nt_dot(a, b):
    return lax.dot_general(a, b, (((1,), (1,)), ((), ())), preferred_element_type=F32)


def kernel(groups, scale, rank, ids_ref, x_ref, wg, wu, wd, ag, au, ad, bg, bu, bd, out_ref,
           wbuf, sbuf, dbuf, acc, low, lowm, lowd, xs, hid,
           xsend, xrecv, lsend, lrecv, osend, orecv,
           wsem, ssem, dsem, xs_sem, xr_sem, ls_sem, lr_sem, os_sem, or_sem):
    me = lax.axis_index("data")
    tok, d = x_ref.shape
    ff = wd.shape[0]
    na = ag.shape[0]
    per_owner = na // rank
    cap = xsend.shape[2]
    rows = groups * cap
    nq, nf, nn = d // KC, ff // FT, d // NT
    nw = 2 * nq

    barrier = pltpu.get_barrier_semaphore()
    for j in range(1, groups):
        pl.semaphore_signal(barrier, inc=1, device_id={"data": lax.rem(me + j, groups)}, device_id_type=MESH)

    def w_copy(i, p, q):
        src = (wg, wu)[p]
        slot = lax.rem(i, W_SLOTS)
        return pltpu.make_async_copy(src.at[pl.ds(q * KC, KC), :], wbuf.at[slot], wsem.at[slot])

    def s_copy_a(p, q):
        slot = 2 * q + p
        return pltpu.make_async_copy((ag, au)[p].at[:, pl.ds(q * KC, KC)], sbuf.at[slot], ssem.at[slot])

    def s_copy_f(t, f):
        slot = lax.rem(2 * nq + 3 * f + t, S_SLOTS)
        return pltpu.make_async_copy((bg, bu, ad)[t].at[:, pl.ds(f * FT, FT)], sbuf.at[slot], ssem.at[slot])

    def s_copy_b(m):
        slot = lax.rem(2 * nq + 3 * nf + m, S_SLOTS)
        return pltpu.make_async_copy(bd.at[:, pl.ds(m * FT, FT)], sbuf.at[slot], ssem.at[slot])

    nb = d // FT

    def s_issue(b):
        k = b - 2 * nq
        for t in range(3):
            @pl.when(jnp.logical_and(k < 3 * nf, lax.rem(k, 3) == t))
            def _():
                s_copy_f(t, k // 3).start()

        @pl.when(jnp.logical_and(k >= 3 * nf, k < 3 * nf + nb))
        def _():
            s_copy_b(k - 3 * nf).start()

    def d_copy(n):
        slot = lax.rem(n, D_SLOTS)
        return pltpu.make_async_copy(wd.at[:, pl.ds(n * NT, NT)], dbuf.at[slot], dsem.at[slot])

    for q in range(nq):
        for p in range(2):
            s_copy_a(p, q).start()
            if 2 * q + p < W_SLOTS:
                w_copy(2 * q + p, p, q).start()
    for b in range(2 * nq, S_SLOTS):
        s_copy_f((b - 2 * nq) % 3, (b - 2 * nq) // 3).start()

    ids_row = ids_ref[...]
    own_row = ids_row // per_owner
    ti = lax.broadcasted_iota(jnp.int32, (tok, tok), 0)
    tj = lax.broadcasted_iota(jnp.int32, (tok, tok), 1)
    eye = ti == tj
    ids_col = jnp.sum(jnp.where(eye, ids_row, 0), axis=1, keepdims=True)
    own_col = ids_col // per_owner
    same = own_col == own_row
    arr_row = jnp.sum(jnp.where(jnp.logical_and(same, ti < tj), 1, 0), axis=0, keepdims=True)
    arr_col = jnp.sum(jnp.where(jnp.logical_and(same, tj < ti), 1, 0), axis=1, keepdims=True)
    slot_row = own_row * cap + arr_row
    slot_col = own_col * cap + arr_col
    pick = (lax.broadcasted_iota(jnp.int32, (rows, tok), 0) == slot_row).astype(F32).astype(BF16)
    back = (lax.broadcasted_iota(jnp.int32, (tok, rows), 1) == slot_col).astype(F32).astype(BF16)
    loc = jnp.broadcast_to((ids_col - own_col * per_owner).astype(F32), (tok, 128)).astype(BF16)
    lsend[...] = jnp.dot(pick, loc, preferred_element_type=F32).reshape(groups, cap, 128).astype(BF16)
    for q in range(nq):
        part = jnp.dot(pick, x_ref[:, q * KC:(q + 1) * KC], preferred_element_type=F32)
        xsend[q] = part.reshape(groups, cap, KC).astype(BF16)

    pl.semaphore_wait(barrier, groups - 1)

    def l_copy(j):
        to = lax.rem(me + j, groups)
        return pltpu.make_async_remote_copy(lsend.at[to], lrecv.at[me], ls_sem.at[j], lr_sem.at[j], device_id={"data": to}, device_id_type=MESH)

    def x_copy(q, j):
        to = lax.rem(me + j, groups)
        return pltpu.make_async_remote_copy(xsend.at[q, to], xrecv.at[q, me], xs_sem.at[q, j], xr_sem.at[q, j], device_id={"data": to}, device_id_type=MESH)

    def o_copy(n, j):
        to = lax.rem(me + j, groups)
        return pltpu.make_async_remote_copy(osend.at[n, to], orecv.at[n, me], os_sem.at[n, j], or_sem.at[n, j], device_id={"data": to}, device_id_type=MESH)

    for j in range(1, groups):
        l_copy(j).start()
    for q in range(nq):
        for j in range(1, groups):
            x_copy(q, j).start()
    lrecv[me] = lsend[me]
    for q in range(nq):
        xrecv[q, me] = xsend[q, me]

    low[...] = jnp.zeros_like(low)
    acc[...] = jnp.zeros_like(acc)
    lowd[...] = jnp.zeros_like(lowd)

    def k_step(q, carry):
        for j in range(1, groups):
            x_copy(q, j).wait_recv()
        xq = xrecv[q].astype(F32).reshape(rows, KC).astype(BF16)
        xs[q] = xq
        for p in range(2):
            i = 2 * q + p
            slot = lax.rem(i, W_SLOTS)
            s_copy_a(p, q).wait()
            low[p] += nt_dot(xq, sbuf[i])
            s_issue(i + S_SLOTS)
            w_copy(i, p, q).wait()
            for n in range(nf):
                cols = slice(n * FT, (n + 1) * FT)
                acc[p, :, cols] += jnp.dot(xq, wbuf[slot, :, cols], preferred_element_type=F32)
            nxt = i + W_SLOTS
            pn = (p + W_SLOTS) % 2

            @pl.when(nxt < nw)
            def _():
                w_copy(nxt, pn, nxt // 2).start()
        return carry

    lax.fori_loop(0, nq, k_step, 0)

    for j in range(1, groups):
        l_copy(j).wait_recv()
    loc_in = lrecv[...].astype(F32).reshape(rows, 128)
    lane_ad = (lax.broadcasted_iota(jnp.int32, (rows, 128), 1) // rank).astype(F32)

    def keep_own(v):
        parts = []
        for c in range(na // 128):
            own = loc_in == lane_ad + float(c * (128 // rank))
            parts.append(jnp.where(own, v[:, c * 128:(c + 1) * 128], 0.0).astype(BF16))
        return jnp.concatenate(parts, axis=1)

    for p in range(2):
        lowm[p] = keep_own(low[p])

    def f_step(f, carry):
        pre = []
        cols = pl.ds(pl.multiple_of(f * FT, FT), FT)
        for p in range(2):
            s_copy_f(p, f).wait()
            b = 2 * nq + 3 * f + p
            slot = lax.rem(b, S_SLOTS)
            delta = (scale * jnp.dot(lowm[p], sbuf[slot], preferred_element_type=F32)).astype(BF16)
            pre.append(acc[p, :, cols] + delta.astype(F32))
            s_issue(b + S_SLOTS)
        h = (jax.nn.silu(pre[0]) * pre[1]).astype(BF16)
        hid[:, cols] = h
        s_copy_f(2, f).wait()
        b = 2 * nq + 3 * f + 2
        lowd[...] += nt_dot(h, sbuf[lax.rem(b, S_SLOTS)])
        s_issue(b + S_SLOTS)

        @pl.when(jnp.logical_and(lax.rem(f, 2) == 0, f // 2 < D_SLOTS))
        def _():
            d_copy(f // 2).start()
        return carry

    lax.fori_loop(0, nf, f_step, 0)
    lowm[0] = keep_own(lowd[...])

    per_b = FT // NT

    def n_step(n, carry):
        m = n // per_b
        slot = lax.rem(2 * nq + 3 * nf + m, S_SLOTS)

        @pl.when(lax.rem(n, per_b) == 0)
        def _():
            s_copy_b(m).wait()
        bcols = pl.ds(pl.multiple_of(lax.rem(n, per_b) * NT, NT), NT)
        delta = (scale * jnp.dot(lowm[0], sbuf[slot, :, bcols], preferred_element_type=F32)).astype(BF16)
        d_copy(n).wait()
        ds = lax.rem(n, D_SLOTS)
        base = jnp.dot(hid[...], dbuf[ds], preferred_element_type=F32)
        xcols = pl.ds(pl.multiple_of(lax.rem(n, KC // NT) * NT, NT), NT)
        res = xs[n // (KC // NT), :, xcols].astype(F32) + (base + delta.astype(F32))
        osend[n] = res.reshape(groups, cap, NT).astype(BF16)
        for j in range(1, groups):
            o_copy(n, j).start()

        @pl.when(n + D_SLOTS < nn)
        def _():
            d_copy(n + D_SLOTS).start()
        orecv[n, me] = osend[n, me]
        return carry

    lax.fori_loop(0, nn, n_step, 0)

    for n in range(nn):
        for j in range(1, groups):
            o_copy(n, j).wait_recv()
        got = orecv[n].astype(F32).reshape(rows, NT).astype(BF16)
        out_ref[:, n * NT:(n + 1) * NT] = jnp.dot(back, got, preferred_element_type=F32).astype(BF16)

    for j in range(1, groups):
        l_copy(j).wait_send()
        for q in range(nq):
            x_copy(q, j).wait_send()
        for n in range(nn):
            o_copy(n, j).wait_send()


def solution(mesh):
    groups = mesh.shape["data"]
    row_spec = P(("rep", "data"), None)
    id_spec = P(("rep", "data"))
    owned_spec = P("data", None, None)

    def device_step(x, adapter_id, w_gate, w_up, w_down, a_gate, b_gate, a_up, b_up, a_down, b_down):
        tok, d = x.shape
        ff = w_gate.shape[1]
        per_owner, rank = a_gate.shape[:2]
        na = per_owner * rank
        cap = (3 * tok + groups - 1) // groups
        rows = groups * cap
        nq, nn = d // KC, d // NT

        def flat(a):
            return a.reshape(na, a.shape[2])

        hbm = pl.BlockSpec(memory_space=pl.ANY)
        vmem = pl.BlockSpec(memory_space=pltpu.VMEM)
        dma = pltpu.SemaphoreType.DMA
        return pl.pallas_call(
            functools.partial(kernel, groups, LORA_ALPHA / rank, rank),
            out_shape=jax.ShapeDtypeStruct((tok, d), BF16),
            in_specs=[vmem, vmem] + [hbm] * 9,
            out_specs=vmem,
            scratch_shapes=[
                pltpu.VMEM((W_SLOTS, KC, ff), BF16),
                pltpu.VMEM((S_SLOTS, na, FT), BF16),
                pltpu.VMEM((D_SLOTS, ff, NT), BF16),
                pltpu.VMEM((2, rows, ff), F32),
                pltpu.VMEM((2, rows, na), F32),
                pltpu.VMEM((2, rows, na), BF16),
                pltpu.VMEM((rows, na), F32),
                pltpu.VMEM((nq, rows, KC), BF16),
                pltpu.VMEM((rows, ff), BF16),
                pltpu.VMEM((nq, groups, cap, KC), BF16),
                pltpu.VMEM((nq, groups, cap, KC), BF16),
                pltpu.VMEM((groups, cap, 128), BF16),
                pltpu.VMEM((groups, cap, 128), BF16),
                pltpu.VMEM((nn, groups, cap, NT), BF16),
                pltpu.VMEM((nn, groups, cap, NT), BF16),
                dma((W_SLOTS,)), dma((S_SLOTS,)), dma((D_SLOTS,)),
                dma((nq, groups)), dma((nq, groups)),
                dma((groups,)), dma((groups,)),
                dma((nn, groups)), dma((nn, groups)),
            ],
            compiler_params=pltpu.CompilerParams(collective_id=0, has_side_effects=True, vmem_limit_bytes=67043328),
            name="lora_layer",
        )(adapter_id.reshape(1, tok), x, w_gate, w_up, w_down, flat(a_gate), flat(a_up), flat(a_down), flat(b_gate), flat(b_up), flat(b_down))

    return jax.shard_map(device_step, mesh=mesh, in_specs=(row_spec, id_spec, P(), P(), P(), owned_spec, owned_spec, owned_spec, owned_spec, owned_spec, owned_spec), out_specs=row_spec, check_vma=False)
```

time: 271 us -> 59.3 us (0.22); the launches traced: 266 us -> 59.2 us
  matrix products: 105 us -> 0 us
  local copies, waits for them, and re-layouts: 72.7 us -> 1.67 us
  Pallas kernels: 0 us -> 57.5 us
  waiting for transfers between devices: 39.2 us -> 0 us
  starting transfers between devices: 26.5 us -> 0 us
  blocking collectives: 15.7 us -> 0 us
  other arithmetic: 5.74 us -> 0 us
    dot_general x14 -> x0, matrix products: 105 us -> none  [the longest x3 32.1 us: value_a9(): jnp.einsum('md,mrd->mr', tok_rows, a_rows, preferred_element_type=jnp.flo...]
    gather x6 -> x0, local copies, waits for them, and re-layouts: 71.4 us -> none  [the longest x3 37.5 us: value_a9(): b_rows = jnp.take(b_mat, row_ids, axis=0)]
    pallas_call x0 -> x1, Pallas kernels: none -> 57.5 us  [device_step(): pl.pallas_call(functools.partial(kernel, groups, LORA_ALPHA / rank, rank)...]
    all_to_all x5 -> x0, waiting for transfers between devices: 39.2 us -> none  [the longest x1 25.2 us: device_step(): lax.all_to_all(value_a9(recv_x, recv_ids, a_up, b_up), 'data', 0, 0, tile...]
    all_to_all x5 -> x0, starting transfers between devices: 26.5 us -> none  [the longest x1 6.01 us: device_step(): recv_ids = lax.all_to_all(send_ids, 'data', 0, 0, tiled=True)]
    all_to_all x1 -> x0, blocking collectives: 15.7 us -> none  [device_step(): lax.all_to_all(value_a9(recv_h, recv_ids, a_down, b_down), 'data', 0, 0,...]
    convert_element_type x7 -> x0, other arithmetic: 4.02 us -> none  [the longest x3 3.89 us: value_a9(): return (array_b10 * full_rows).astype(jnp.bfloat16)]
  transfers between devices with their start and end apart: 5 -> 0, of which waited for: 4 -> 0; matrix products, arithmetic and copies ran while one was open for 36% -> 0% of each run, Pallas kernels for 0% -> 0%
where the time goes in v1:
time: 59.3 us; the launch traced here: 59.2 us
  Pallas kernels  57.5 us (97%)
  local copies, waits for them, and re-layouts  1.67 us (3%)
    pallas_call x1, Pallas kernels, device_step(): pl.pallas_call(functools.partial(kernel, groups, LORA_ALPHA / rank, rank)...  57.5 us
    unnamed x1, local copies, waits for them, and re-layouts  1.67 us

profile of v1, /device:TPU:81, one launch (start us, length us, event | category | flops | bytes accessed | tf_op | source)
XLA Modules:
  0.0 59.2 jit_solution(14104704213812174959)
XLA Ops:
  0.0 57.5 %lora_layer.1 = bf16[64,2048]{1,0:T(8,128)(2,1)} custom-call(s32[1,64]{1,0:T(1,128)} %bitcast.13, bf16[64,2048]{1,0:T(8,128)(2,1)} %x_ref.1, bf16[2048,5632]{1,0:T(8,128)(2,1)} %wg.1, bf16[2048,5632]{1,0:T(8,128)(2,1)} %wu.1, bf16[5632,2048]{1,0:T(8,128)(2,1)} %wd.1, bf16[1024,2048]{1,0:T(8,128)(2,1)} %bitcast.10, bf16[1024,2048]{1,0:T(8,128)(2,1)} %bitcast.11, ...), custom_call_target="tpu_custom_call" | custom-call | tf_op jit(solution)/shard_map/lora_layer/pallas_call | solution.py:262
  57.5 1.7 %copy.13 = bf16[64,2048]{1,0:T(8,128)(2,1)} copy(bf16[64,2048]{1,0:T(8,128)(2,1)} %lora_layer.1) | data formatting | bytes 524288

commit v2 on v0

v2 whole, which is shorter than its diff:
```python
import functools

import jax
import jax.numpy as jnp
from jax import lax
from jax.experimental import pallas as pl
from jax.experimental.pallas import tpu as pltpu
from jax.sharding import PartitionSpec as P

LORA_ALPHA = 32
F32 = jnp.float32
BF16 = jnp.bfloat16
MESH = pl.DeviceIdType.MESH

KB = 512
VMEM_LIMIT = 67043328


def nt_dot(a, b):
    return lax.dot_general(a, b, (((1,), (1,)), ((), ())), preferred_element_type=F32)


def kernel(groups, scale, rank, ids_hbm, x_hbm, wg, wu, wd, ag, au, ad, bg, bu, bd, out_ref,
           ids_ref, x_ref, pool, acc, low, lowd, lowm, xs, hid, xsend, xrecv, lsend, lrecv, osend, orecv,
           w_sem, g_sem, in_sem, xs_sem, xr_sem, ls_sem, lr_sem, os_sem, or_sem):
    me = lax.axis_index("data")
    partner = me + 1 - 2 * lax.rem(me, 2)
    tok, d = x_hbm.shape
    nf, ra = wd.shape[0], ag.shape[0]
    na = ra * KB
    per_owner = na // rank
    cap = xsend.shape[2]
    rows = groups * cap
    slots = pool.shape[0]
    nq = nm = d // KB

    peers = [lax.rem(base + 4, groups) for base in (me, partner)]
    peers += [lax.rem(me + 2, groups), lax.rem(me + 6, groups), lax.rem(partner + 2, groups), lax.rem(partner + 6, groups), partner]
    assert groups == 8
    links = range(groups - 1)

    barrier = pltpu.get_barrier_semaphore()
    for to in peers:
        pl.semaphore_signal(barrier, inc=1, device_id={"data": to}, device_id_type=MESH)
    ids_copy = pltpu.make_async_copy(ids_hbm, ids_ref, in_sem.at[0])
    x_in = pltpu.make_async_copy(x_hbm, x_ref, in_sem.at[1])
    ids_copy.start()
    x_in.start()

    per_k = 2 * (nf + ra)
    per_f = 3 * ra
    per_m = nf + ra
    f_base = nq * per_k
    per_b = 2 * ra
    m_base = f_base + nf * per_f
    d_base = m_base + nm * ra
    total = d_base + nm * nf

    def slot_of(i):
        return i % slots if isinstance(i, int) else lax.rem(i, slots)

    ring = slots // per_k
    assert slots % per_k == 0

    def w_block(q, p, n):
        s = slot_of(q * per_k + p * nf + n)
        return pltpu.make_async_copy((wg, wu)[p].at[pl.ds(q * KB, KB), pl.ds(n * KB, KB)], pool.at[s], w_sem.at[q % ring if isinstance(q, int) else lax.rem(q, ring)])

    def w_wait(q):
        s = slot_of(q * per_k)
        every = pool.at[pl.ds(s, 2 * nf)]
        pltpu.make_async_copy(every, every, w_sem.at[q % ring if isinstance(q, int) else lax.rem(q, ring)]).wait()

    def group(src, c, i):
        count = src.shape[0]
        s = slot_of(i)
        if isinstance(s, int):
            assert s + count <= slots
        return pltpu.make_async_copy(src.at[:, :, pl.ds(c * KB, KB)], pool.at[pl.ds(s, count)], g_sem.at[s])

    def a_group(q, p):
        return group((ag, au)[p], q, q * per_k + 2 * nf + p * ra)

    def b_at(f, p):
        return f_base + (p * ra if isinstance(f, int) and f == 0 else f * per_f - ra + p * ra)

    def b_group(f, p):
        return group((bg, bu)[p], f, b_at(f, p))

    def ad_at(f):
        return m_base - ra if isinstance(f, int) and f == nf - 1 else f_base + (f + 1) * per_f + per_b - ra

    def ad_group(f):
        return group(ad, f, ad_at(f))

    def bd_group(m):
        return group(bd, m, m_base + m * ra)

    def wd_group(m):
        return group(wd, m, d_base + m * nf)

    later = [(b_at(f, p), ra, b_group(f, p)) for f in range(nf) for p in range(2)]
    later += [(ad_at(f), ra, ad_group(f)) for f in range(nf)]
    later += [(m_base + m * ra, ra, bd_group(m)) for m in range(nm)]
    later += [(d_base + m * nf, nf, wd_group(m)) for m in range(nm)]
    later.sort(key=lambda t: t[0])
    assert [t[0] for t in later] == [f_base + sum(t[1] for t in later[:k]) for k in range(len(later))]

    def k_start(q):
        for p in range(2):
            for n in range(nf):
                w_block(q, p, n).start()
            a_group(q, p).start()

    def start_between(lo, hi):
        for i, count, copy in later:
            if lo <= i + count - 1 - slots < hi:
                copy.start()

    k_start(0)

    ids_copy.wait()
    ids_row = ids_ref[...]
    own_row = ids_row // per_owner
    ti = lax.broadcasted_iota(jnp.int32, (tok, tok), 0)
    tj = lax.broadcasted_iota(jnp.int32, (tok, tok), 1)
    eye = ti == tj
    ids_col = jnp.sum(jnp.where(eye, ids_row, 0), axis=1, keepdims=True)
    own_col = ids_col // per_owner
    same = own_col == own_row
    arr_row = jnp.sum(jnp.where(jnp.logical_and(same, ti < tj), 1, 0), axis=0, keepdims=True)
    arr_col = jnp.sum(jnp.where(jnp.logical_and(same, tj < ti), 1, 0), axis=1, keepdims=True)
    slot_row = own_row * cap + arr_row
    slot_col = own_col * cap + arr_col
    pick = (lax.broadcasted_iota(jnp.int32, (rows, tok), 0) == slot_row).astype(F32).astype(BF16)
    back = (lax.broadcasted_iota(jnp.int32, (tok, rows), 1) == slot_col).astype(F32).astype(BF16)
    loc = jnp.broadcast_to((ids_col - own_col * per_owner).astype(F32), (tok, 128)).astype(BF16)
    lsend[...] = jnp.dot(pick, loc, preferred_element_type=F32).reshape(groups, cap, 128).astype(BF16)
    x_in.wait()
    for q in range(nq):
        part = jnp.dot(pick, x_ref[:, q * KB:(q + 1) * KB], preferred_element_type=F32)
        xsend[q] = part.reshape(groups, cap, KB).astype(BF16)

    pl.semaphore_wait(barrier, groups - 1)

    def remote(src, dst, j, send_sem, recv_sem):
        return pltpu.make_async_remote_copy(src.at[peers[j]], dst.at[me], send_sem.at[j], recv_sem.at[j], device_id={"data": peers[j]}, device_id_type=MESH)

    def l_copy(j):
        return remote(lsend, lrecv, j, ls_sem, lr_sem)

    def x_copy(q, j):
        return remote(xsend.at[q], xrecv.at[q], j, xs_sem.at[q], xr_sem.at[q])

    def o_copy(m, j):
        return remote(osend.at[m], orecv.at[m], j, os_sem.at[m], or_sem.at[m])

    for q in range(nq):
        for j in links:
            x_copy(q, j).start()
    for j in links:
        l_copy(j).start()
    for q in range(1, ring):
        k_start(q)
    lrecv[me] = lsend[me]
    for q in range(nq):
        xrecv[q, me] = xsend[q, me]

    low[...] = jnp.zeros_like(low)
    acc[...] = jnp.zeros_like(acc)
    lowd[...] = jnp.zeros_like(lowd)

    def k_in(q):
        for j in links:
            x_copy(q, j).wait_recv()
        xq = xrecv[q].astype(F32).reshape(rows, KB).astype(BF16)
        xs[q] = xq
        for p in range(2):
            a_group(q, p).wait()
        w_wait(q)
        return xq

    def k_low(q, xq):
        for p in range(2):
            for r in range(ra):
                low[p, r] += nt_dot(pool[slot_of(q * per_k + 2 * nf + p * ra) + r], xq)

    def k_base(q, xq):
        s0 = slot_of(q * per_k)
        for p in range(2):
            for n in range(nf):
                acc[p, n] += jnp.dot(xq, pool[s0 + p * nf + n], preferred_element_type=F32)

    def k_step(q, carry):
        xq = k_in(q)
        k_low(q, xq)
        k_base(q, xq)
        for z in range(nq - 1):
            @pl.when(q == z)
            def _():
                if z + ring < nq:
                    k_start(z + ring)
                start_between(z * per_k, (z + 1) * per_k)
        return carry

    lax.fori_loop(0, nq - 1, k_step, 0)

    xq = k_in(nq - 1)
    for j in links:
        l_copy(j).wait_recv()
    loc_in = lrecv[...].astype(F32).reshape(rows, 128).astype(BF16)
    lane0 = (lax.broadcasted_iota(jnp.int32, (8, 128), 1) == 0).astype(F32).astype(BF16)
    loc_row = nt_dot(lane0, loc_in)[0:1, :]
    ad_col = (lax.broadcasted_iota(jnp.int32, (KB, rows), 0) // rank).astype(F32)
    unit = (lax.broadcasted_iota(jnp.int32, (rows, rows), 0) == lax.broadcasted_iota(jnp.int32, (rows, rows), 1)).astype(F32).astype(BF16)

    def keep_own(v, r):
        own = ad_col + float(r * (KB // rank)) == loc_row
        kept = jnp.where(own, v, 0.0).astype(BF16)
        return nt_dot(unit, kept).astype(BF16)

    k_low(nq - 1, xq)
    for p in range(2):
        for r in range(ra):
            lowm[p, r] = keep_own(low[p, r], r)
    k_base(nq - 1, xq)
    start_between((nq - 1) * per_k, nq * per_k)
    for j in links:
        l_copy(j).wait_send()
        for q in range(nq):
            x_copy(q, j).wait_send()

    def low_dot(p, i0):
        full = jnp.dot(lowm[p, 0], pool[slot_of(i0)], preferred_element_type=F32)
        for r in range(1, ra):
            full += jnp.dot(lowm[p, r], pool[slot_of(i0) + r], preferred_element_type=F32)
        return (scale * full).astype(BF16).astype(F32)

    def hidden(f):
        g = acc[0, f] + low_dot(0, b_at(f, 0))
        u = acc[1, f] + low_dot(1, b_at(f, 1))
        return (jax.nn.silu(g) * u).astype(BF16)

    def low_down(f):
        for r in range(ra):
            lowd[r] += nt_dot(pool[slot_of(ad_at(f)) + r], hid[f])

    for p in range(2):
        b_group(0, p).wait()
    hid[0] = hidden(0)
    start_between(f_base, f_base + per_b)

    def f_step(g, carry):
        steps = [pair * g + 1 + z for z in range(pair)]
        for f in steps:
            for p in range(2):
                b_group(f, p).wait()
            ad_group(f - 1).wait()
        for f in steps:
            h = hidden(f)
            low_down(f - 1)
            hid[f] = h
        for z in range((nf - 1) // pair):
            @pl.when(g == z)
            def _():
                lo = f_base + per_b + z * pair * per_f
                start_between(lo, lo + pair * per_f)
        return carry

    pair = 2 if nf % 2 == 1 else 1
    lax.fori_loop(0, (nf - 1) // pair, f_step, 0)
    assert m_base - ra + slots >= total

    def m_in(m):
        bd_group(m).wait()
        wd_group(m).wait()

    def m_base_dot(m):
        s0 = slot_of(d_base + m * nf)
        base = jnp.dot(hid[0], pool[s0], preferred_element_type=F32)
        for k in range(1, nf):
            base += jnp.dot(hid[k], pool[s0 + k], preferred_element_type=F32)
        return base

    def m_out(m, base):
        res = xs[m].astype(F32) + (base + low_dot(0, m_base + m * ra))
        osend[m] = res.reshape(groups, cap, KB).astype(BF16)
        for j in links:
            o_copy(m, j).start()
        orecv[m, me] = osend[m, me]

    ad_group(nf - 1).wait()
    m_in(0)
    low_down(nf - 1)
    base = m_base_dot(0)
    for r in range(ra):
        lowm[0, r] = keep_own(lowd[r], r)
    m_out(0, base)

    def m_step(m, carry):
        m_in(m)
        m_out(m, m_base_dot(m))
        return carry

    lax.fori_loop(1, nm, m_step, 0)

    for m in range(nm):
        for j in links:
            o_copy(m, j).wait_recv()
            o_copy(m, j).wait_send()
        got = orecv[m].astype(F32).reshape(rows, KB).astype(BF16)
        out_ref[:, m * KB:(m + 1) * KB] = jnp.dot(back, got, preferred_element_type=F32).astype(BF16)


def solution(mesh):
    groups = mesh.shape["data"]
    row_spec = P(("rep", "data"), None)
    id_spec = P(("rep", "data"))
    owned_spec = P("data", None, None)

    def device_step(x, adapter_id, w_gate, w_up, w_down, a_gate, b_gate, a_up, b_up, a_down, b_down):
        tok, d = x.shape
        ff = w_gate.shape[1]
        per_owner, rank = a_gate.shape[:2]
        na = per_owner * rank
        cap = (3 * tok + groups - 1) // groups
        rows = groups * cap
        nq, nf, ra = d // KB, ff // KB, na // KB
        slots = 3 * 2 * (nf + ra)

        def flat(a):
            return a.reshape(-1, KB, a.shape[-1])

        hbm = pl.BlockSpec(memory_space=pl.ANY)
        vmem = pl.BlockSpec(memory_space=pltpu.VMEM)
        dma = pltpu.SemaphoreType.DMA
        return pl.pallas_call(
            functools.partial(kernel, groups, LORA_ALPHA / rank, rank),
            out_shape=jax.ShapeDtypeStruct((tok, d), BF16),
            in_specs=[hbm] * 11,
            out_specs=vmem,
            scratch_shapes=[
                pltpu.VMEM((1, tok), jnp.int32),
                pltpu.VMEM((tok, d), BF16),
                pltpu.VMEM((slots, KB, KB), BF16),
                pltpu.VMEM((2, nf, rows, KB), F32),
                pltpu.VMEM((2, ra, KB, rows), F32),
                pltpu.VMEM((ra, KB, rows), F32),
                pltpu.VMEM((2, ra, rows, KB), BF16),
                pltpu.VMEM((nq, rows, KB), BF16),
                pltpu.VMEM((nf, rows, KB), BF16),
                pltpu.VMEM((nq, groups, cap, KB), BF16),
                pltpu.VMEM((nq, groups, cap, KB), BF16),
                pltpu.VMEM((groups, cap, 128), BF16),
                pltpu.VMEM((groups, cap, 128), BF16),
                pltpu.VMEM((nq, groups, cap, KB), BF16),
                pltpu.VMEM((nq, groups, cap, KB), BF16),
                dma((3,)), dma((slots,)), dma((2,)),
                dma((nq, groups)), dma((nq, groups)),
                dma((groups,)), dma((groups,)),
                dma((nq, groups)), dma((nq, groups)),
            ],
            compiler_params=pltpu.CompilerParams(collective_id=0, has_side_effects=True, vmem_limit_bytes=VMEM_LIMIT),
            name="lora_layer",
        )(adapter_id.reshape(1, tok), x, w_gate, w_up, flat(w_down), flat(a_gate), flat(a_up), flat(a_down), flat(b_gate), flat(b_up), flat(b_down))

    return jax.shard_map(device_step, mesh=mesh, in_specs=(row_spec, id_spec, P(), P(), P(), owned_spec, owned_spec, owned_spec, owned_spec, owned_spec, owned_spec), out_specs=row_spec, check_vma=False)
```

time: 271 us -> 52.1 us (0.19); the launches traced: 266 us -> 52 us
  matrix products: 105 us -> 0 us
  local copies, waits for them, and re-layouts: 72.7 us -> 1.67 us
  Pallas kernels: 0 us -> 50.3 us
  waiting for transfers between devices: 39.2 us -> 0 us
  starting transfers between devices: 26.5 us -> 0 us
  blocking collectives: 15.7 us -> 0 us
  other arithmetic: 5.74 us -> 0 us
    dot_general x14 -> x0, matrix products: 105 us -> none  [the longest x3 32.1 us: value_a9(): jnp.einsum('md,mrd->mr', tok_rows, a_rows, preferred_element_type=jnp.flo...]
    gather x6 -> x0, local copies, waits for them, and re-layouts: 71.4 us -> none  [the longest x3 37.5 us: value_a9(): b_rows = jnp.take(b_mat, row_ids, axis=0)]
    pallas_call x0 -> x1, Pallas kernels: none -> 50.3 us  [device_step(): pl.pallas_call(functools.partial(kernel, groups, LORA_ALPHA / rank, rank)...]
    all_to_all x5 -> x0, waiting for transfers between devices: 39.2 us -> none  [the longest x1 25.2 us: device_step(): lax.all_to_all(value_a9(recv_x, recv_ids, a_up, b_up), 'data', 0, 0, tile...]
    all_to_all x5 -> x0, starting transfers between devices: 26.5 us -> none  [the longest x1 6.01 us: device_step(): recv_ids = lax.all_to_all(send_ids, 'data', 0, 0, tiled=True)]
    all_to_all x1 -> x0, blocking collectives: 15.7 us -> none  [device_step(): lax.all_to_all(value_a9(recv_h, recv_ids, a_down, b_down), 'data', 0, 0,...]
    convert_element_type x7 -> x0, other arithmetic: 4.02 us -> none  [the longest x3 3.89 us: value_a9(): return (array_b10 * full_rows).astype(jnp.bfloat16)]
  transfers between devices with their start and end apart: 5 -> 0, of which waited for: 4 -> 0; matrix products, arithmetic and copies ran while one was open for 36% -> 0% of each run, Pallas kernels for 0% -> 0%
where the time goes in v2:
time: 52.1 us; the launch traced here: 52 us
  Pallas kernels  50.3 us (97%)
  local copies, waits for them, and re-layouts  1.67 us (3%)
    pallas_call x1, Pallas kernels, device_step(): pl.pallas_call(functools.partial(kernel, groups, LORA_ALPHA / rank, rank)...  50.3 us
    unnamed x1, local copies, waits for them, and re-layouts  1.67 us

profile of v2, /device:TPU:81, one launch (start us, length us, event | category | flops | bytes accessed | tf_op | source)
XLA Modules:
  0.0 52.0 jit_solution(17122226031273177299)
XLA Ops:
  0.0 50.3 %lora_layer.1 = bf16[64,2048]{1,0:T(8,128)(2,1)} custom-call(s32[1,64]{1,0:T(1,128)} %bitcast.15, bf16[64,2048]{1,0:T(8,128)(2,1)} %x_hbm.1, bf16[2048,5632]{1,0:T(8,128)(2,1)} %wg.1, bf16[2048,5632]{1,0:T(8,128)(2,1)} %wu.1, bf16[11,512,2048]{2,1,0:T(8,128)(2,1)} %bitcast.8, bf16[2,512,2048]{2,1,0:T(8,128)(2,1)} %bitcast.12, ...), custom_call_target="tpu_custom_call" | custom-call | tf_op jit(solution)/shard_map/lora_layer/pallas_call | solution.py:337
  50.3 1.7 %copy.13 = bf16[64,2048]{1,0:T(8,128)(2,1)} copy(bf16[64,2048]{1,0:T(8,128)(2,1)} %lora_layer.1) | data formatting | bytes 524288

commit v3 on v2

--- a/solution.py
+++ b/solution.py
@@ -53,8 +53,7 @@
     f_base = nq * per_k
     per_b = 2 * ra
     m_base = f_base + nf * per_f
-    d_base = m_base + nm * ra
-    total = d_base + nm * nf
+    total = m_base + nm * per_m
 
     def slot_of(i):
         return i % slots if isinstance(i, int) else lax.rem(i, slots)
@@ -94,28 +93,28 @@
         return group(ad, f, ad_at(f))
 
     def bd_group(m):
-        return group(bd, m, m_base + m * ra)
+        return group(bd, m, m_base + m * per_m)
 
     def wd_group(m):
-        return group(wd, m, d_base + m * nf)
+        return group(wd, m, m_base + m * per_m + ra)
 
     later = [(b_at(f, p), ra, b_group(f, p)) for f in range(nf) for p in range(2)]
     later += [(ad_at(f), ra, ad_group(f)) for f in range(nf)]
-    later += [(m_base + m * ra, ra, bd_group(m)) for m in range(nm)]
-    later += [(d_base + m * nf, nf, wd_group(m)) for m in range(nm)]
+    later += [(m_base + m * per_m, ra, bd_group(m)) for m in range(nm)]
+    later += [(m_base + m * per_m + ra, nf, wd_group(m)) for m in range(nm)]
     later.sort(key=lambda t: t[0])
     assert [t[0] for t in later] == [f_base + sum(t[1] for t in later[:k]) for k in range(len(later))]
 
     def k_start(q):
         for p in range(2):
             for n in range(nf):
-                w_block(q, p, n).start()
-            a_group(q, p).start()
+                w_block(q, p, n).start(priority=1)
+            a_group(q, p).start(priority=1)
 
     def start_between(lo, hi):
         for i, count, copy in later:
             if lo <= i + count - 1 - slots < hi:
-                copy.start()
+                copy.start(priority=1)
 
     k_start(0)
 
@@ -185,16 +184,16 @@
             for r in range(ra):
                 low[p, r] += nt_dot(pool[slot_of(q * per_k + 2 * nf + p * ra) + r], xq)
 
-    def k_base(q, xq):
+    def k_base(q, xq, lo, hi):
         s0 = slot_of(q * per_k)
         for p in range(2):
-            for n in range(nf):
+            for n in range(lo, hi):
                 acc[p, n] += jnp.dot(xq, pool[s0 + p * nf + n], preferred_element_type=F32)
 
     def k_step(q, carry):
         xq = k_in(q)
         k_low(q, xq)
-        k_base(q, xq)
+        k_base(q, xq, 0, nf)
         for z in range(nq - 1):
             @pl.when(q == z)
             def _():
@@ -205,7 +204,20 @@
 
     lax.fori_loop(0, nq - 1, k_step, 0)
 
+    def low_dot(p, i0):
+        full = jnp.dot(lowm[p, 0], pool[slot_of(i0)], preferred_element_type=F32)
+        for r in range(1, ra):
+            full += jnp.dot(lowm[p, r], pool[slot_of(i0) + r], preferred_element_type=F32)
+        return (scale * full).astype(BF16).astype(F32)
+
+    def hidden(f):
+        g = acc[0, f] + low_dot(0, b_at(f, 0))
+        u = acc[1, f] + low_dot(1, b_at(f, 1))
+        return (jax.nn.silu(g) * u).astype(BF16)
+
     xq = k_in(nq - 1)
+    for p in range(2):
+        b_group(0, p).wait()
     for j in links:
         l_copy(j).wait_recv()
     loc_in = lrecv[...].astype(F32).reshape(rows, 128).astype(BF16)
@@ -220,35 +232,22 @@
         return nt_dot(unit, kept).astype(BF16)
 
     k_low(nq - 1, xq)
+    k_base(nq - 1, xq, 0, nf // 3)
     for p in range(2):
         for r in range(ra):
             lowm[p, r] = keep_own(low[p, r], r)
-    k_base(nq - 1, xq)
-    start_between((nq - 1) * per_k, nq * per_k)
+    k_base(nq - 1, xq, nf // 3, 2 * nf // 3)
+    hid[0] = hidden(0)
+    k_base(nq - 1, xq, 2 * nf // 3, nf)
+    start_between((nq - 1) * per_k, f_base + per_b)
     for j in links:
         l_copy(j).wait_send()
         for q in range(nq):
             x_copy(q, j).wait_send()
 
-    def low_dot(p, i0):
-        full = jnp.dot(lowm[p, 0], pool[slot_of(i0)], preferred_element_type=F32)
-        for r in range(1, ra):
-            full += jnp.dot(lowm[p, r], pool[slot_of(i0) + r], preferred_element_type=F32)
-        return (scale * full).astype(BF16).astype(F32)
-
-    def hidden(f):
-        g = acc[0, f] + low_dot(0, b_at(f, 0))
-        u = acc[1, f] + low_dot(1, b_at(f, 1))
-        return (jax.nn.silu(g) * u).astype(BF16)
-
     def low_down(f):
         for r in range(ra):
             lowd[r] += nt_dot(pool[slot_of(ad_at(f)) + r], hid[f])
-
-    for p in range(2):
-        b_group(0, p).wait()
-    hid[0] = hidden(0)
-    start_between(f_base, f_base + per_b)
 
     def f_step(g, carry):
         steps = [pair * g + 1 + z for z in range(pair)]
@@ -276,14 +275,14 @@
         wd_group(m).wait()
 
     def m_base_dot(m):
-        s0 = slot_of(d_base + m * nf)
+        s0 = slot_of(m_base + m * per_m + ra)
         base = jnp.dot(hid[0], pool[s0], preferred_element_type=F32)
         for k in range(1, nf):
             base += jnp.dot(hid[k], pool[s0 + k], preferred_element_type=F32)
         return base
 
     def m_out(m, base):
-        res = xs[m].astype(F32) + (base + low_dot(0, m_base + m * ra))
+        res = xs[m].astype(F32) + (base + low_dot(0, m_base + m * per_m))
         osend[m] = res.reshape(groups, cap, KB).astype(BF16)
         for j in links:
             o_copy(m, j).start()

time: 52.1 us -> 49.7 us (0.954)
  Pallas kernels: 50.3 us -> 47.9 us
    pallas_call x1, Pallas kernels: 50.3 us -> 47.9 us  [device_step(): pl.pallas_call(functools.partial(kernel, groups, LORA_ALPHA / rank, rank)...]
where the time goes in v3:
time: 49.7 us; the launch traced here: 49.6 us
  Pallas kernels  47.9 us (96%)
  local copies, waits for them, and re-layouts  1.67 us (3%)
    pallas_call x1, Pallas kernels, device_step(): pl.pallas_call(functools.partial(kernel, groups, LORA_ALPHA / rank, rank)...  47.9 us
    unnamed x1, local copies, waits for them, and re-layouts  1.67 us

profile of v3, /device:TPU:81, one launch (start us, length us, event | category | flops | bytes accessed | tf_op | source)
XLA Modules:
  0.0 49.6 jit_solution(18043929498522379883)
XLA Ops:
  0.0 47.9 %lora_layer.1 = bf16[64,2048]{1,0:T(8,128)(2,1)} custom-call(s32[1,64]{1,0:T(1,128)} %bitcast.15, bf16[64,2048]{1,0:T(8,128)(2,1)} %x_hbm.1, bf16[2048,5632]{1,0:T(8,128)(2,1)} %wg.1, bf16[2048,5632]{1,0:T(8,128)(2,1)} %wu.1, bf16[11,512,2048]{2,1,0:T(8,128)(2,1)} %bitcast.8, bf16[2,512,2048]{2,1,0:T(8,128)(2,1)} %bitcast.12, ...), custom_call_target="tpu_custom_call" | custom-call | tf_op jit(solution)/shard_map/lora_layer/pallas_call | solution.py:336
  47.9 1.7 %copy.13 = bf16[64,2048]{1,0:T(8,128)(2,1)} copy(bf16[64,2048]{1,0:T(8,128)(2,1)} %lora_layer.1) | data formatting | bytes 524288
